TPU v7x, 32 devices: a whole 2x2x4 slice. The times are simulated.
32 devices in a mesh: cp: 8 (over z, y), fsdp: 4 (over x, core).
Axes of the slice: x: 2, y: 2, z: 4, core: 2. Of those that a mesh axis runs over, the one named last changes fastest.
Arguments:
- query_states: bfloat16 [4, 1024, 1024], P('fsdp', 'cp'), may hold values from -32 to 32
- key_states: bfloat16 [4, 1024, 1024], P('fsdp', 'cp'), may hold values from -32 to 32
- value_states: bfloat16 [4, 1024, 1024], P('fsdp', 'cp'), may hold values from -6 to 6
- span_order: int32 [16], replicated, may hold values from 0 to 15, as said below
- block_mask: int32 [16, 16], replicated, may hold values from 0 to 1, as said below
- output_weight: bfloat16 [1024, 2048], P(('cp', 'fsdp')), may hold values from -0.1875 to 0.1875
- upstream: bfloat16 [4, 1024, 2048], P('fsdp', 'cp'), may hold values from -6 to 6
Outputs:
- projected: bfloat16 [4, 1024, 2048], P('fsdp', 'cp')
- query_gradient: bfloat16 [4, 1024, 1024], P('fsdp', 'cp')
- key_gradient: bfloat16 [4, 1024, 1024], P('fsdp', 'cp')
- value_gradient: bfloat16 [4, 1024, 1024], P('fsdp', 'cp')
- weight_gradient: float32 [1024, 2048], P(('cp', 'fsdp'))
Inputs may be any that keep to these rules, and one draw needn't show every extreme that they name: `span_order`: entries 2 d and 2 d + 1 hold positions p and 15 - p; every position appears once. `block_mask`: the diagonal is 1.
All inputs are finite; a program needn't handle non-finite values.
Results may differ from a plain program's by a relative error of at most 0.024.
Values may be sent and summed in bfloat16 or wider, within the bound.
A program may use at most 128 MiB of HBM per device.

v0:
```python
import math

import jax
import jax.numpy as jnp
from jax import lax
from jax.sharding import PartitionSpec as P

HEADS = 8
HEAD = 128


lowest = -1e30


def split_heads(row_block):
    return row_block.reshape(row_block.shape[0], HEADS, HEAD)


def pair_scores(query_rows, key_rows):
    return jnp.einsum(
        "qhd,khd->hqk",
        split_heads(query_rows),
        split_heads(key_rows),
        preferred_element_type=jnp.float32,
    ) * (1.0 / HEAD)


def storage_mask(span_order, block_mask):
    span_count = span_order.shape[0]
    onehot = (span_order[:, None] == jnp.arange(span_count, dtype=jnp.int32)[None, :]).astype(
        jnp.float32
    )
    permuted = jnp.dot(jnp.dot(onehot, block_mask.astype(jnp.float32)), onehot.T)
    return permuted > 0.5


def allowed_block(span_ok, positions, query_begin, query_total, key_begin, key_total, span_rows):
    span_sub = lax.dynamic_slice(
        span_ok,
        (query_begin // span_rows, key_begin // span_rows),
        (query_total // span_rows, key_total // span_rows),
    )
    spread = jnp.broadcast_to(
        span_sub[:, None, :, None],
        (query_total // span_rows, span_rows, key_total // span_rows, span_rows),
    )
    spread = spread.reshape(query_total, key_total)
    query_pos = lax.dynamic_slice_in_dim(positions, query_begin, query_total)
    key_pos = lax.dynamic_slice_in_dim(positions, key_begin, key_total)
    return spread & (key_pos[None, :] <= query_pos[:, None])


def local_terms(query_rows, grad_rows, log_rows, delta_rows, key_rows, value_rows, allowed):
    scores = pair_scores(query_rows, key_rows)
    probability = jnp.where(allowed[None], jnp.exp(scores - log_rows[..., None]), 0.0)
    dprob = jnp.einsum(
        "qhd,khd->hqk",
        split_heads(grad_rows),
        split_heads(value_rows),
        preferred_element_type=jnp.float32,
    )
    dscores = (probability * (dprob - delta_rows[..., None]) * (1.0 / HEAD)).astype(jnp.bfloat16)
    return (probability, dscores)


def local(query_states, key_states, value_states, span_order, block_mask, output_weight, upstream):
    query_rows = query_states[0]
    key_local = key_states[0]
    value_local = value_states[0]
    upstream_rows = upstream[0]
    tokens = query_rows.shape[0]
    span_rows = tokens // 2
    positions = (
        span_order[:, None] * span_rows + jnp.arange(span_rows, dtype=jnp.int32)[None, :]
    ).reshape(-1)
    span_ok = storage_mask(span_order, block_mask)
    own_start = lax.axis_index("cp") * tokens
    key_all, value_all = (
        lax.all_gather(key_local, "cp", axis=0, tiled=True),
        lax.all_gather(value_local, "cp", axis=0, tiled=True),
    )
    weight = lax.all_gather(output_weight, ("cp", "fsdp"), axis=0, tiled=True)
    length = key_all.shape[0]
    key_block = math.gcd(length, 512)
    block_count = length // key_block
    block_steps = jnp.arange(block_count, dtype=jnp.int32)

    def stats_step(running, step_index):
        key_begin = step_index * key_block
        key_rows = lax.dynamic_slice_in_dim(key_all, key_begin, key_block)
        allowed = allowed_block(
            span_ok, positions, own_start, tokens, key_begin, key_block, span_rows
        )
        maxima, totals = running
        scores = pair_scores(query_rows, key_rows)
        masked = jnp.where(allowed[None], scores, lowest)
        new_max = jnp.maximum(maxima, masked.max(-1))
        exp_terms = jnp.where(allowed[None], jnp.exp(scores - new_max[..., None]), 0.0)
        return ((new_max, totals * jnp.exp(maxima - new_max) + exp_terms.sum(-1)), None)

    stat_start = (
        jnp.full((HEADS, tokens), lowest, jnp.float32),
        jnp.zeros((HEADS, tokens), jnp.float32),
    )
    (maxima, totals), _ = lax.scan(stats_step, stat_start, block_steps)
    log_total = maxima + jnp.log(totals)

    def output_step(attn_sum, step_index):
        key_begin = step_index * key_block
        key_rows = lax.dynamic_slice_in_dim(key_all, key_begin, key_block)
        value_rows = lax.dynamic_slice_in_dim(value_all, key_begin, key_block)
        allowed = allowed_block(
            span_ok, positions, own_start, tokens, key_begin, key_block, span_rows
        )
        scores = pair_scores(query_rows, key_rows)
        probability = jnp.where(allowed[None], jnp.exp(scores - log_total[..., None]), 0.0)
        return (
            attn_sum
            + jnp.einsum(
                "hqk,khd->qhd",
                probability.astype(jnp.bfloat16),
                split_heads(value_rows),
                preferred_element_type=jnp.float32,
            ),
            None,
        )

    zero_heads = jnp.zeros((tokens, HEADS, HEAD), jnp.float32)
    attn_sum, _ = lax.scan(output_step, zero_heads, block_steps)
    attended = lax.optimization_barrier(attn_sum.reshape(tokens, -1).astype(jnp.bfloat16))
    projected = jnp.dot(attended, weight, preferred_element_type=jnp.float32).astype(jnp.bfloat16)
    grad_attended = lax.dot_general(
        upstream_rows, weight, (((1,), (1,)), ((), ())), preferred_element_type=jnp.float32
    ).astype(jnp.bfloat16)
    grad_attended = lax.optimization_barrier(grad_attended)
    weight_term = lax.dot_general(
        attended, upstream_rows, (((0,), (0,)), ((), ())), preferred_element_type=jnp.float32
    )
    row_delta = (
        (grad_attended.astype(jnp.float32) * attended.astype(jnp.float32))
        .reshape(tokens, HEADS, HEAD)
        .sum(-1)
    )
    delta_heads = row_delta.T

    def query_step(grad_sum, step_index):
        key_begin = step_index * key_block
        key_rows = lax.dynamic_slice_in_dim(key_all, key_begin, key_block)
        value_rows = lax.dynamic_slice_in_dim(value_all, key_begin, key_block)
        allowed = allowed_block(
            span_ok, positions, own_start, tokens, key_begin, key_block, span_rows
        )
        probability, dscores = local_terms(
            query_rows, grad_attended, log_total, delta_heads, key_rows, value_rows, allowed
        )
        return (
            grad_sum
            + jnp.einsum(
                "hqk,khd->qhd", dscores, split_heads(key_rows), preferred_element_type=jnp.float32
            ),
            None,
        )

    query_sum, _ = lax.scan(query_step, zero_heads, block_steps)
    query_gradient = query_sum.reshape(tokens, -1).astype(jnp.bfloat16)
    log_all, delta_all = (
        lax.all_gather(log_total.T, "cp", axis=0, tiled=True),
        lax.all_gather(row_delta, "cp", axis=0, tiled=True),
    )
    sums_now = (zero_heads, zero_heads)
    query_piece = lax.all_gather(query_rows, "cp", axis=0, tiled=True)
    grad_piece = lax.all_gather(grad_attended, "cp", axis=0, tiled=True)
    row_count = query_piece.shape[0]
    sources = row_count // tokens
    group_size = math.gcd(sources, max(1, 512 // tokens))
    group_rows = group_size * tokens

    def group_step(running, step_index):
        offset = step_index * group_rows
        query_group = lax.dynamic_slice_in_dim(query_piece, offset, group_rows)
        grad_group = lax.dynamic_slice_in_dim(grad_piece, offset, group_rows)
        log_group = lax.dynamic_slice_in_dim(log_all, offset, group_rows).T
        delta_group = lax.dynamic_slice_in_dim(delta_all, offset, group_rows).T
        allowed = allowed_block(
            span_ok, positions, offset, group_rows, own_start, tokens, span_rows
        )
        key_sum, value_sum = running
        probability, dscores = local_terms(
            query_group, grad_group, log_group, delta_group, key_local, value_local, allowed
        )
        probability_low = probability.astype(jnp.bfloat16).reshape(
            HEADS, group_size, tokens, tokens
        )
        dscores_group = dscores.reshape(HEADS, group_size, tokens, tokens)
        qsplit = query_group.reshape(group_size, tokens, HEADS, HEAD)
        gsplit = grad_group.reshape(group_size, tokens, HEADS, HEAD)
        key_part = jnp.einsum(
            "hgqk,gqhd->gkhd", dscores_group, qsplit, preferred_element_type=jnp.float32
        ).astype(jnp.bfloat16)
        value_part = jnp.einsum(
            "hgqk,gqhd->gkhd", probability_low, gsplit, preferred_element_type=jnp.float32
        ).astype(jnp.bfloat16)
        key_part, value_part = lax.optimization_barrier((key_part, value_part))
        return (
            (
                key_sum + key_part.astype(jnp.float32).sum(0),
                value_sum + value_part.astype(jnp.float32).sum(0),
            ),
            None,
        )

    sums_now, _ = lax.scan(group_step, sums_now, jnp.arange(sources // group_size, dtype=jnp.int32))
    key_sum, value_sum = sums_now
    key_gradient = key_sum.reshape(tokens, -1).astype(jnp.bfloat16)
    value_gradient = value_sum.reshape(tokens, -1).astype(jnp.bfloat16)
    cycle_count = lax.axis_size("cp")
    batch_count = lax.axis_size("fsdp")
    slab_rows = weight_term.shape[0] // (cycle_count * batch_count)
    reordered = weight_term.reshape(cycle_count, batch_count, slab_rows, -1).transpose(1, 0, 2, 3)
    reordered = reordered.reshape(weight_term.shape[0], -1)
    partial_batch = lax.psum_scatter(
        reordered.astype(jnp.bfloat16), "fsdp", scatter_dimension=0, tiled=True
    )
    weight_gradient = lax.psum_scatter(partial_batch, "cp", scatter_dimension=0, tiled=True).astype(
        jnp.float32
    )
    return (
        projected[None],
        query_gradient[None],
        key_gradient[None],
        value_gradient[None],
        weight_gradient,
    )


def solution(mesh):
    return jax.shard_map(
        local,
        mesh=mesh,
        in_specs=(
            P("fsdp", "cp", None),
            P("fsdp", "cp", None),
            P("fsdp", "cp", None),
            P(),
            P(),
            P(("cp", "fsdp"), None),
            P("fsdp", "cp", None),
        ),
        out_specs=(
            P("fsdp", "cp", None),
            P("fsdp", "cp", None),
            P("fsdp", "cp", None),
            P("fsdp", "cp", None),
            P(("cp", "fsdp"), None),
        ),
        check_vma=False,
    )
```

profile of v0, /device:TPU:0, one launch (start us, length us, event | category | flops | bytes accessed | tf_op | source)
XLA Modules:
  0.0 406.9 jit_solution(1121399911245663614)
XLA Ops:
  7.2 1.8 copy.109
  13.7 50.0 %all-gather.15.cloned.1.call-done = bf16[1,1024,1024]{1,2,0:T(8,128)(2,1)} async-done(((bf16[1,128,1024]{1,2,0:T(8,128)(2,1)}), bf16[1,1024,1024]{1,2,0:T(8,128)(2,1)}) %all-gather.15.cloned.1.call-update) | async-done | bytes 2097168 | tf_op jit(solution)/shard_map/all_gather | solution.py:79
  63.8 9.1 %while.60 = (s32[]{:T(128)}, f32[8,128]{1,0:T(8,128)S(1)}, f32[8,128]{1,0:T(8,128)S(1)}, s32[2]{0:T(128)S(1)}, pred[16,16]{1,0:T(8,128)(4,1)S(1)}, /*index=5*/s3...) while((s32[]{:T(128)}, f32[8,128]{1,0:T(8,128)S(1)}, ...), condition=%wide.region_3.4_spmd.clone, body=%wide.region_0.3_spmd.clone.sunk | while | flops 138023952 | bytes 9825273 | solution.py:105
  72.9 42.0 %all-gather.13.cloned.1.call-done = bf16[1,1024,1024]{1,2,0:T(8,128)(2,1)} async-done(((bf16[1,128,1024]{1,2,0:T(8,128)(2,1)}), bf16[1,1024,1024]{1,2,0:T(8,128)(2,1)}) %all-gather.13.cloned.1.call-update) | async-done | bytes 2097168 | tf_op jit(solution)/shard_map/all_gather | solution.py:80
  114.9 12.2 %while.61 = (s32[]{:T(128)}, f32[128,8,128]{0,2,1:T(8,128)}, s32[2]{0:T(128)S(1)}, bf16[1024,1024]{0,1:T(8,128)(2,1)}, pred[16,16]{1,0:T(8,128)(4,1)S(1)}, /*ind...) while((s32[]{:T(128)}, f32[128,8,128]{0,2,1:T(8,128)}, ...), condition=%wide.region_5.6_spmd.clone, body=%wide.region_4.5_spmd.clone.sunk | while | flops 270925856 | bytes 9710592 | solution.py:129
  124.4 2.8 fusion.106
  129.9 2.3 copy.120
  134.0 43.7 %all-gather.9.cloned.1.call-done = bf16[1024,2048]{1,0:T(8,128)(2,1)} async-done(((bf16[32,2048]{1,0:T(8,128)(2,1)}), bf16[1024,2048]{1,0:T(8,128)(2,1)}) %all-gather.9.cloned.1.call-update) | async-done | bytes 4194320 | tf_op jit(solution)/shard_map/all_gather | solution.py:82
  177.7 4.4 %convolution_convert_fusion.3 = bf16[128,1024]{1,0:T(8,128)(2,1)} fusion(bf16[1024,2048]{1,0:T(8,128)(2,1)} %all-gather.9.cloned.1.call-done, bf16[1,128,2048]{2,1,0:T(8,128)(2,1)S(1)} %copy-done), kind=kOutput, calls=%fused_computation.74 | convolution fusion | flops 537001984 | bytes 4980736 | tf_op jit(solution)/shard_map/dot_general | solution.py:132
  182.9 32.3 %all_gather.25 = f32[1024,8]{0,1:T(8,128)} all-gather(f32[128,8]{0,1:T(8,128)S(1)} %bitcast.269), channel_id=1, replica_groups=mesh['cp'=8,'fsdp'=4] {'cp'}, dimensions={0}, use_global_device_ids=true | all-gather | bytes 36864 | tf_op jit(solution)/shard_map/all_gather | solution.py:167
  219.7 27.5 %while.62 = (s32[]{:T(128)}, f32[128,8,128]{0,2,1:T(8,128)}, s32[2]{0:T(128)}, bf16[1024,1024]{0,1:T(8,128)(2,1)S(1)}, pred[16,16]{1,0:T(8,128)(4,1)S(1)}, /*ind...) while((s32[]{:T(128)}, f32[128,8,128]{0,2,1:T(8,128)}, ...), condition=%wide.region_8.9_spmd.clone, body=%wide.region_7.8_spmd.clone.sunk | while | flops 406716416 | bytes 18365456 | solution.py:164
  221.6 2.4 constant_dynamic-slice_fusion.14
  229.1 4.2 %fusion.114 = f32[128,8,128]{0,2,1:T(8,128)} fusion(bf16[512,8,128]{0,2,1:T(8,128)(2,1)} %bitcast.244, f32[8,512,128]{2,1,0:T(8,128)} %fusion.113, bf16[512,8,128]{0,2,1:T(8,128)(2,1)} %bitcast.250, f32[8,128]{1,0:T(8,128)} %get-tuple-element.1869, f32[8,128]{1,0:T(8,128)S(1)} %get-tuple-element.1866, pred[128,512]{0,1:T(8,128)(4,1)S(1)} %copy.203, ...), kind=kOutput, calls=%fused_computation.34.clone.1 | convolution fusion | flops 272367616 | bytes 5578753 | tf_op jit(solution)/shard_map/while/body/eval_jaxpr/hqk,khd->qhd/dot_general | solution.py:158
  235.3 2.4 constant_dynamic-slice_fusion.14
  242.8 4.4 %fusion.114 = f32[128,8,128]{0,2,1:T(8,128)} fusion(bf16[512,8,128]{0,2,1:T(8,128)(2,1)} %bitcast.244, f32[8,512,128]{2,1,0:T(8,128)} %fusion.113, bf16[512,8,128]{0,2,1:T(8,128)(2,1)} %bitcast.250, f32[8,128]{1,0:T(8,128)} %get-tuple-element.1869, f32[8,128]{1,0:T(8,128)S(1)} %get-tuple-element.1866, pred[128,512]{0,1:T(8,128)(4,1)S(1)} %copy.203, ...), kind=kOutput, calls=%fused_computation.34.clone.1 | convolution fusion | flops 272367616 | bytes 5578753 | tf_op jit(solution)/shard_map/while/body/eval_jaxpr/hqk,khd->qhd/dot_general | solution.py:158
  249.2 33.7 %all_gather.27 = f32[1024,8]{1,0:T(8,128)S(1)} all-gather(f32[128,8]{1,0:T(8,128)} %copy-done.14), channel_id=1, replica_groups=mesh['cp'=8,'fsdp'=4] {'cp'}, dimensions={0}, use_global_device_ids=true | all-gather | bytes 36864 | tf_op jit(solution)/shard_map/all_gather | solution.py:168
  283.0 3.7 fusion.46
  286.8 45.5 %all-gather.11.cloned.1.call-done = bf16[1024,1024]{1,0:T(8,128)(2,1)} async-done(((bf16[128,1024]{1,0:T(8,128)(2,1)}), bf16[1024,1024]{1,0:T(8,128)(2,1)}) %all-gather.11.cloned.1.call-update) | async-done | bytes 2097168 | tf_op jit(solution)/shard_map/all_gather | solution.py:172
  332.3 41.2 %while.63 = (s32[]{:T(128)}, f32[128,8,128]{0,2,1:T(8,128)S(1)}, f32[128,8,128]{0,2,1:T(8,128)}, s32[2]{0:T(128)S(1)}, bf16[1024,1024]{0,1:T(8,128)(2,1)}, /*ind...) while((s32[]{:T(128)}, f32[128,8,128]{0,2,1:T(8,128)S(1)}, ...), condition=%wide.region_12.13_spmd.clone, body=%wide.region_9.12_spmd.clone.sunk | while | flops 544604160 | bytes 55680168 | solution.py:212
  339.3 2.1 fusion.122
  344.0 2.3 multiply_convert_fusion.2
  359.9 2.1 fusion.122
  364.6 2.4 multiply_convert_fusion.2
  376.3 22.1 %reduce-scatter.5.cloned.1.call-done = bf16[32,2048]{1,0:T(8,128)(2,1)} async-done(((bf16[256,2048]{1,0:T(8,128)(2,1)}), bf16[32,2048]{1,0:T(8,128)(2,1)}) %reduce-scatter.5.cloned.1.call-update) | async-done | bytes 131088 | tf_op jit(solution)/shard_map/reduce_scatter | solution.py:224
  (206 shorter events, 79.8 us)
Async XLA Ops:
  7.2 121.4 %copy-start = (bf16[1,128,2048]{2,1,0:T(8,128)(2,1)S(1)}, bf16[1,128,2048]{2,1,0:T(8,128)(2,1)}, u32[]{:S(2)}) copy-start(bf16[1,128,2048]{2,1,0:T(8,128)(2,1)} %param.21) | copy-start | bytes 1572868
  7.2 56.6 %all-gather.15.cloned.1.call-start = ((), (), s32[]{:S(2)}) async-start(), calls=%async_computation.7 | async-start | bytes 2359296 | tf_op jit(solution)/shard_map/all_gather | solution.py:79
  9.1 105.8 %all-gather.13.cloned.1.call-start = ((), (), s32[]{:S(2)}) async-start(), calls=%async_computation.6 | async-start | bytes 2359296 | tf_op jit(solution)/shard_map/all_gather | solution.py:80
  11.0 166.8 %all-gather.9.cloned.1.call-start = ((), (), s32[]{:S(2)}) async-start(), calls=%async_computation.2 | async-start | bytes 4325376 | tf_op jit(solution)/shard_map/all_gather | solution.py:82
  11.7 275.0 %reduce-scatter.3.cloned.1.call-start = ((), (), s32[]{:S(2)}) async-start(), calls=%async_computation.4 | async-start | bytes 5242880 | tf_op jit(solution)/shard_map/reduce_scatter | solution.py:221
  63.8 3.4 copy-start.5
  68.3 3.4 copy-start.5
  116.2 2.6 copy-start.6
  121.8 2.6 copy-start.6
  128.4 1.4 copy-start.12
  132.2 154.6 %all-gather.17.cloned.1.call-start = ((), (), s32[]{:S(2)}) async-start(), calls=%async_computation.8 | async-start | bytes 2359296 | tf_op jit(solution)/shard_map/all_gather | solution.py:171
  134.0 198.3 %all-gather.11.cloned.1.call-start = ((), (), s32[]{:S(2)}) async-start(), calls=%async_computation.3 | async-start | bytes 2359296 | tf_op jit(solution)/shard_map/all_gather | solution.py:172
  182.2 37.5 %copy-start.1 = (bf16[1024,1024]{0,1:T(8,128)(2,1)S(1)}, bf16[1024,1024]{0,1:T(8,128)(2,1)}, u32[]{:S(2)}) copy-start(bf16[1024,1024]{0,1:T(8,128)(2,1)} %get-tuple-element.1953) | copy-start | bytes 6291460
  182.2 216.2 %reduce-scatter.5.cloned.1.call-start = ((), (), s32[]{:S(2)}) async-start(), calls=%async_computation.5 | async-start | bytes 1179648 | tf_op jit(solution)/shard_map/reduce_scatter | solution.py:224
  218.4 1.3 copy-start.14
  247.2 35.8 %copy-start.13 = (bf16[128,1024]{1,0:T(8,128)(2,1)S(1)}, bf16[128,1024]{1,0:T(8,128)(2,1)}, u32[]{:S(2)}) copy-start(bf16[128,1024]{1,0:T(8,128)(2,1)} %copy-done.12) | copy-start | bytes 786436
  339.3 2.1 copy-start.10
  341.3 2.6 copy-start.11
  344.0 2.4 copy-start.2
  348.9 1.9 copy-start.4
  359.8 2.1 copy-start.10
  361.9 2.6 copy-start.11
  364.6 2.4 copy-start.2
  369.5 1.9 copy-start.4
  (7 other events, 6.6 us)
Sparse Core Ops, SparseCore 0:
  10.6 53.1 all-gather.14
  66.4 48.5 all-gather.12
  117.8 59.8 all-gather.8
  180.1 43.3 reduce-scatter.2
  226.0 55.8 all-gather.16
  284.5 47.7 all-gather.10
  335.7 62.6 reduce-scatter.4
where the time goes:
time: 408 us; the launch traced here: 407 us
  waiting for transfers between devices  204 us (50%)
  blocking collectives  66 us (16%)
  local copies, waits for them, and re-layouts  59.5 us (15%)
  matrix products  43.6 us (11%)
  between operations  14.3 us (4%)
  other arithmetic  12.9 us (3%)
  loops' own time  6.1 us (1%)
    all_gather x1, waiting for transfers between devices, local(): lax.all_gather(key_local, 'cp', axis=0, tiled=True)  50 us
    all_gather x1, waiting for transfers between devices, local(): grad_piece = lax.all_gather(grad_attended, 'cp', axis=0, tiled=True)  45.5 us
    all_gather x1, waiting for transfers between devices, local(): weight = lax.all_gather(output_weight, ('cp', 'fsdp'), axis=0, tiled=True)  43.7 us
    all_gather x1, waiting for transfers between devices, local(): lax.all_gather(value_local, 'cp', axis=0, tiled=True)  42 us
    all_gather x1, blocking collectives, local(): lax.all_gather(row_delta, 'cp', axis=0, tiled=True)  33.7 us
    all_gather x1, blocking collectives, local(): lax.all_gather(log_total.T, 'cp', axis=0, tiled=True)  32.3 us
    reduce_scatter x1, waiting for transfers between devices, local(): lax.psum_scatter(partial_batch, 'cp', scatter_dimension=0, tiled=True)  22.1 us
    dot_general x6, matrix products, pair_scores(): jnp.einsum('qhd,khd->hqk', split_heads(query_rows), split_heads(key_rows)...  8.95 us
  transfers between devices with their start and end apart: 7, of which 5 were waited for; matrix products, arithmetic and copies ran while one was open for 26% of the time, Pallas kernels for 0%

commit v1 on v0

--- a/solution.py
+++ b/solution.py
@@ -3,6 +3,8 @@
 import jax
 import jax.numpy as jnp
 from jax import lax
+from jax.experimental import pallas as pl
+from jax.experimental.pallas import tpu as pltpu
 from jax.sharding import PartitionSpec as P
 
 HEADS = 8
@@ -233,9 +235,316 @@
     )
 
 
+MESH = pl.DeviceIdType.MESH
+
+
+def remote(src, dst, send_sem, recv_sem, device):
+    return pltpu.make_async_remote_copy(
+        src_ref=src,
+        dst_ref=dst,
+        send_sem=send_sem,
+        recv_sem=recv_sem,
+        device_id=device,
+        device_id_type=MESH,
+    )
+
+
+def rows_of(begin, count):
+    return pl.ds(pl.multiple_of(begin, count), count)
+
+
+def greet(devices):
+    barrier = pltpu.get_barrier_semaphore()
+    for device in devices:
+        pl.semaphore_signal(barrier, inc=1, device_id=device, device_id_type=MESH)
+    pl.semaphore_wait(barrier, len(devices))
+
+
+def gather_kernel(
+    n, q, k, v, up, w, qh, kh, vh, ups, wall,
+    local_sem, heads_s, heads_r, ring_s, ring_r, part_s, part_r, cross_s, cross_r, relay_s, relay_r,
+):
+    me = lax.axis_index("cp")
+    col = lax.axis_index("fsdp")
+    partner = {"fsdp": col + 1 - 2 * lax.rem(col, 2)}
+    cross_col = lax.rem(col + 2, 4)
+    cross = {"fsdp": cross_col}
+    tokens = up.shape[0]
+    half = tokens // 2
+    slab = w.shape[0]
+    depth = n // 2
+    zed, why = me // 2, lax.rem(me, 2)
+    place = zed + why * (n - 1 - 2 * zed)
+
+    def at_place(offset):
+        r = lax.rem(place + offset + 2 * n, n)
+        return 2 * r + (r // depth) * (2 * n - 1 - 4 * r)
+
+    def head_cols(d):
+        return rows_of(d * HEAD, HEAD)
+
+    peers = [{"cp": lax.rem(me + i, n)} for i in range(1, n)]
+    greet(peers + [partner, cross])
+
+    def chunk_ref(which, owner):
+        if which == 2:
+            return wall.at[rows_of(owner * (4 * slab) + col * slab, slab)]
+        return ups.at[rows_of(owner * tokens + which * half, half)]
+
+    def own_ref(which):
+        if which == 2:
+            return w
+        return up.at[rows_of(which * half, half)]
+
+    sends = []
+    toward = ({"cp": at_place(1)}, {"cp": at_place(-1)})
+
+    def chunks_at(step, way):
+        if step < depth:
+            return (2, 0, 1)
+        return (2, 0) if way == 0 else (1,)
+
+    def ring_start(step, way, which):
+        owner = at_place((1 - step) if way == 0 else (step - 1))
+        source = own_ref(which) if step == 1 else chunk_ref(which, owner)
+        copy = remote(
+            source, chunk_ref(which, owner),
+            ring_s.at[way, step, which], ring_r.at[way, step, which], toward[way],
+        )
+        copy.start()
+        sends.append(copy)
+
+    def ring_wait(step, way, which):
+        owner = at_place(-step if way == 0 else step)
+        block = chunk_ref(which, owner)
+        remote(
+            block, block, ring_s.at[way, step, which], ring_r.at[way, step, which], toward[way]
+        ).wait_recv()
+
+    spread = []
+
+    def spread_weight(owner, source):
+        slot = len(spread)
+        spread.append(owner)
+        block = chunk_ref(2, owner)
+        for device, ss, rs in ((cross, cross_s, cross_r), (partner, part_s, part_r)):
+            copy = remote(source, block, ss.at[slot], rs.at[slot], device)
+            copy.start()
+            sends.append(copy)
+
+    for way in range(2):
+        for which in chunks_at(1, way):
+            ring_start(1, way, which)
+    triples = ((q, qh), (k, kh), (v, vh))
+    for i in range(1, n):
+        d = lax.rem(me + i, n)
+        for t, (a, b) in enumerate(triples):
+            copy = remote(
+                a.at[:, head_cols(d)], b.at[rows_of(me * tokens, tokens)],
+                heads_s.at[t, i], heads_r.at[t, i], {"cp": d},
+            )
+            copy.start()
+            sends.append(copy)
+    own = [
+        pltpu.make_async_copy(
+            a.at[:, head_cols(me)], b.at[rows_of(me * tokens, tokens)], local_sem.at[t]
+        )
+        for t, (a, b) in enumerate(triples)
+    ]
+    own.append(pltpu.make_async_copy(up, ups.at[rows_of(me * tokens, tokens)], local_sem.at[3]))
+    own.append(pltpu.make_async_copy(w, chunk_ref(2, me), local_sem.at[4]))
+    for copy in own:
+        copy.start()
+    spread_weight(me, w)
+    for step in range(1, depth + 1):
+        for way in range(2):
+            for which in chunks_at(step, way):
+                ring_wait(step, way, which)
+                if step < depth and which in chunks_at(step + 1, way):
+                    ring_start(step + 1, way, which)
+                if which == 2:
+                    owner = at_place(-step if way == 0 else step)
+                    spread_weight(owner, chunk_ref(2, owner))
+    for slot, owner in enumerate(spread):
+        block = wall.at[rows_of(owner * (4 * slab) + cross_col * slab, slab)]
+        remote(block, block, cross_s.at[slot], cross_r.at[slot], cross).wait_recv()
+        copy = remote(block, block, relay_s.at[slot], relay_r.at[slot], partner)
+        copy.start()
+        sends.append(copy)
+    for i in range(1, n):
+        source = lax.rem(me + n - i, n)
+        for t, (a, b) in enumerate(triples):
+            block = b.at[rows_of(source * tokens, tokens)]
+            remote(block, block, heads_s.at[t, i], heads_r.at[t, i], {"cp": source}).wait_recv()
+    near = partner["fsdp"]
+    far = lax.rem(near + 2, 4)
+    for slot, owner in enumerate(spread):
+        for other, ss, rs in ((near, part_s, part_r), (far, relay_s, relay_r)):
+            block = wall.at[rows_of(owner * (4 * slab) + other * slab, slab)]
+            remote(block, block, ss.at[slot], rs.at[slot], partner).wait_recv()
+    for copy in own:
+        copy.wait()
+    for copy in sends:
+        copy.wait_send()
+
+
+def scatter_kernel(n, m, a0, a1, a2, a3, dw, b0, b1, b2, b3, dwr, local_sem, ss, rs, ws, wr):
+    me = lax.axis_index("cp")
+    col = lax.axis_index("fsdp")
+    tokens = b0.shape[0]
+    slab = dwr.shape[1]
+    pairs = ((a0, b0), (a1, b1), (a2, b2), (a3, b3))
+    peers = [{"cp": lax.rem(me + i, n)} for i in range(1, n)]
+    columns = [{"fsdp": lax.rem(col + j, m)} for j in range(1, m)]
+    greet(peers + columns)
+    sends = []
+    for t, (a, b) in enumerate(pairs):
+        for i in range(1, n):
+            d = lax.rem(me + i, n)
+            copy = remote(
+                a.at[rows_of(d * tokens, tokens)], b.at[:, rows_of(me * HEAD, HEAD)],
+                ss.at[t, i], rs.at[t, i], {"cp": d},
+            )
+            copy.start()
+            sends.append(copy)
+    for j in range(1, m):
+        g = lax.rem(col + j, m)
+        copy = remote(
+            dw.at[rows_of(g * slab, slab)], dwr.at[j], ws.at[j], wr.at[j], {"fsdp": g}
+        )
+        copy.start()
+        sends.append(copy)
+    own = [
+        pltpu.make_async_copy(
+            a.at[rows_of(me * tokens, tokens)], b.at[:, rows_of(me * HEAD, HEAD)], local_sem.at[t]
+        )
+        for t, (a, b) in enumerate(pairs)
+    ]
+    own.append(
+        pltpu.make_async_copy(dw.at[rows_of(col * slab, slab)], dwr.at[0], local_sem.at[4])
+    )
+    for copy in own:
+        copy.start()
+    for t, (a, b) in enumerate(pairs):
+        for i in range(1, n):
+            source = lax.rem(me + n - i, n)
+            block = b.at[:, rows_of(source * HEAD, HEAD)]
+            remote(block, block, ss.at[t, i], rs.at[t, i], {"cp": source}).wait_recv()
+    for j in range(1, m):
+        block = dwr.at[j]
+        remote(block, block, ws.at[j], wr.at[j], columns[j - 1]).wait_recv()
+    for copy in own:
+        copy.wait()
+    for copy in sends:
+        copy.wait_send()
+
+
+def attention_kernel(q, k, v, ga, allowed, att, dq, dk, dv, kt, vt, dk_sum, dv_sum):
+    step = pl.program_id(0)
+
+    @pl.when(step == 0)
+    def _():
+        kt[...] = k[...].astype(jnp.float32).T.astype(jnp.bfloat16)
+        vt[...] = v[...].astype(jnp.float32).T.astype(jnp.bfloat16)
+        dk_sum[...] = jnp.zeros_like(dk_sum)
+        dv_sum[...] = jnp.zeros_like(dv_sum)
+
+    f32 = jnp.float32
+    nt = (((1,), (1,)), ((), ()))
+    scores = lax.dot_general(k[...], q[...], nt, preferred_element_type=f32) * (1.0 / HEAD)
+    scores = jnp.where(allowed[...].astype(f32) > 0.5, scores, lowest)
+    top = scores.max(0, keepdims=True)
+    terms = jnp.exp(scores - top)
+    probability = terms * (1.0 / terms.sum(0, keepdims=True))
+    low = probability.astype(jnp.bfloat16)
+    att_t = jnp.dot(vt[...], low, preferred_element_type=f32).astype(jnp.bfloat16).astype(f32)
+    att[...] = att_t.T.astype(jnp.bfloat16)
+    delta = (att_t * ga[...].astype(f32).T).sum(0, keepdims=True)
+    dprob = lax.dot_general(v[...], ga[...], nt, preferred_element_type=f32)
+    ds = (probability * (dprob - delta) * (1.0 / HEAD)).astype(jnp.bfloat16)
+    dq_t = jnp.dot(kt[...], ds, preferred_element_type=f32)
+    dq[...] = dq_t.T.astype(jnp.bfloat16)
+    dk_sum[...] += jnp.dot(ds, q[...], preferred_element_type=f32)
+    dv_sum[...] += jnp.dot(low, ga[...], preferred_element_type=f32)
+
+    @pl.when(step == pl.num_programs(0) - 1)
+    def _():
+        dk[...] = dk_sum[...].astype(jnp.bfloat16)
+        dv[...] = dv_sum[...].astype(jnp.bfloat16)
+
+
+def by_heads(query_states, key_states, value_states, span_order, block_mask, output_weight, upstream):
+    n = lax.axis_size("cp")
+    m = lax.axis_size("fsdp")
+    tokens, width = query_states.shape[1:]
+    length = tokens * n
+    model = upstream.shape[2]
+    slab = output_weight.shape[0]
+    span_rows = tokens // 2
+    bf16 = jnp.bfloat16
+    shape = jax.ShapeDtypeStruct
+    vmem = pl.BlockSpec(memory_space=pltpu.VMEM)
+    anywhere = pl.BlockSpec(memory_space=pl.ANY)
+    dma = pltpu.SemaphoreType.DMA
+    half = n // 2
+    qh, kh, vh, ups, weight = pl.pallas_call(
+        lambda *refs: gather_kernel(n, *refs),
+        out_shape=(shape((length, HEAD), bf16),) * 3
+        + (shape((length, model), bf16), shape((width, model), bf16)),
+        in_specs=[vmem] * 5,
+        out_specs=(anywhere,) * 5,
+        scratch_shapes=[
+            dma((5,)), dma((3, n)), dma((3, n)), dma((2, half + 1, 3)), dma((2, half + 1, 3)),
+        ]
+        + [dma((n,))] * 6,
+        compiler_params=pltpu.CompilerParams(collective_id=0, has_side_effects=True),
+        name="gather",
+    )(query_states[0], key_states[0], value_states[0], upstream[0], output_weight)
+    head_rows = lax.dynamic_slice_in_dim(weight, lax.axis_index("cp") * HEAD, HEAD)
+    ga = lax.dot_general(
+        ups, head_rows, (((1,), (1,)), ((), ())), preferred_element_type=jnp.float32
+    ).astype(bf16)
+    positions = (
+        span_order[:, None] * span_rows + jnp.arange(span_rows, dtype=jnp.int32)[None, :]
+    ).reshape(-1)
+    span_ok = storage_mask(span_order, block_mask)
+    allowed = allowed_block(span_ok, positions, 0, length, 0, length, span_rows)
+    allowed = allowed.T.astype(bf16)
+    block = math.gcd(length, 256)
+    rows = pl.BlockSpec((block, HEAD), lambda i: (i, 0))
+    whole = pl.BlockSpec((length, HEAD), lambda i: (0, 0))
+    att_h, dq_h, dk_h, dv_h = pl.pallas_call(
+        attention_kernel,
+        grid=(length // block,),
+        out_shape=(shape((length, HEAD), bf16),) * 4,
+        in_specs=[rows, whole, whole, rows, pl.BlockSpec((length, block), lambda i: (0, i))],
+        out_specs=(rows, rows, whole, whole),
+        scratch_shapes=[pltpu.VMEM((HEAD, length), bf16)] * 2
+        + [pltpu.VMEM((length, HEAD), jnp.float32)] * 2,
+        compiler_params=pltpu.CompilerParams(dimension_semantics=("arbitrary",)),
+        name="attention",
+    )(qh, kh, vh, ga, allowed)
+    weight_term = lax.dot_general(
+        att_h, ups, (((0,), (0,)), ((), ())), preferred_element_type=jnp.float32
+    ).astype(bf16)
+    attended, dq, dk, dv, pieces = pl.pallas_call(
+        lambda *refs: scatter_kernel(n, m, *refs),
+        out_shape=(shape((tokens, width), bf16),) * 4 + (shape((m, slab, model), bf16),),
+        in_specs=[vmem] * 5,
+        out_specs=(vmem,) * 5,
+        scratch_shapes=[dma((5,)), dma((4, n)), dma((4, n)), dma((m,)), dma((m,))],
+        compiler_params=pltpu.CompilerParams(collective_id=1, has_side_effects=True),
+        name="scatter",
+    )(att_h, dq_h, dk_h, dv_h, weight_term)
+    projected = jnp.dot(attended, weight, preferred_element_type=jnp.float32).astype(bf16)
+    weight_gradient = pieces.astype(jnp.float32).sum(0)
+    return (projected[None], dq[None], dk[None], dv[None], weight_gradient)
+
+
 def solution(mesh):
+    fits = mesh.shape["cp"] == HEADS and mesh.shape["fsdp"] == 4
     return jax.shard_map(
-        local,
+        by_heads if fits else local,
         mesh=mesh,
         in_specs=(
             P("fsdp", "cp", None),

time: 408 us -> 141 us (0.35)
  waiting for transfers between devices: 204 us -> 0 us
  Pallas kernels: 0 us -> 117 us
  blocking collectives: 66 us -> 0 us
  local copies, waits for them, and re-layouts: 59.5 us -> 6.1 us
  matrix products: 43.6 us -> 13 us
  between operations: 14.3 us -> 0.71 us
  other arithmetic: 12.9 us -> 3.68 us
  loops' own time: 6.1 us -> 0 us
    all_gather x5 -> x0, waiting for transfers between devices: 181 us -> none  [the longest x1 50 us: local(): lax.all_gather(key_local, 'cp', axis=0, tiled=True)]
    pallas_call x0 -> x3, Pallas kernels: none -> 117 us  [the longest x1 78.3 us: by_heads(): pl.pallas_call(lambda *refs: gather_kernel(n, *refs), out_shape=(shape((l...]
    all_gather x2 -> x0, blocking collectives: 66 us -> none  [the longest x1 33.7 us: local(): lax.all_gather(row_delta, 'cp', axis=0, tiled=True)]
    dot_general x19 -> x3, matrix products: 42.6 us -> 12 us  [the longest x1 4.27 us: by_heads(): lax.dot_general(ups, head_rows, (((1,), (1,)), ((), ())), preferred_eleme...]
    dynamic_slice x37 -> x0, local copies, waits for them, and re-layouts: 27.3 us -> none  [the longest x8 6.01 us: local(): (maxima, totals), _ = lax.scan(stats_step, stat_start, block_steps)]
    reduce_scatter x2 -> x0, waiting for transfers between devices: 22.1 us -> none  [the longest x1 22.1 us: local(): lax.psum_scatter(partial_batch, 'cp', scatter_dimension=0, tiled=True)]
    while x48 -> x0, local copies, waits for them, and re-layouts: 7.25 us -> none
    another operation x4 -> x0, loops' own time: 6.1 us -> none  [the longest x1 1.68 us: local(): lax.scan(group_step, sums_now, jnp.arange(sources // group_size, dtype=jn...]
  transfers between devices with their start and end apart: 7 -> 0, of which waited for: 5 -> 0; matrix products, arithmetic and copies ran while one was open for 26% -> 0% of each run, Pallas kernels for 0% -> 0%
where the time goes in v1:
time: 141 us
  Pallas kernels  117 us (83%)
  matrix products  13 us (9%)
  local copies, waits for them, and re-layouts  6.1 us (4%)
  other arithmetic  3.68 us (3%)
    pallas_call x1, Pallas kernels, by_heads(): pl.pallas_call(lambda *refs: gather_kernel(n, *refs), out_shape=(shape((l...  78.3 us
    pallas_call x1, Pallas kernels, by_heads(): pl.pallas_call(lambda *refs: scatter_kernel(n, m, *refs), out_shape=(shap...  29.7 us
    pallas_call x1, Pallas kernels, by_heads(): pl.pallas_call(attention_kernel, grid=(length // block,), out_shape=(shap...  9.26 us
    dot_general x1, matrix products, by_heads(): lax.dot_general(ups, head_rows, (((1,), (1,)), ((), ())), preferred_eleme...  4.27 us
    dot_general x1, matrix products, by_heads(): jnp.dot(attended, weight, preferred_element_type=jnp.float32).astype(bf16)  3.88 us
    dot_general x1, matrix products, by_heads(): lax.dot_general(att_h, ups, (((0,), (0,)), ((), ())), preferred_element_t...  3.82 us
    reshape x1, local copies, waits for them, and re-layouts, allowed_block(): spread = spread.reshape(query_total, key_total)  3.2 us

profile of v1, /device:TPU:0, one launch (start us, length us, event | category | flops | bytes accessed | tf_op | source)
XLA Modules:
  0.0 140.8 jit_solution(4213822352792318712)
XLA Ops:
  0.6 0.7 broadcast_multiply_fusion
  1.3 1.0 fusion.5
  2.3 0.1 copy.12
  2.4 0.1 iota_add_fusion
  2.5 0.1 add.31
  2.6 0.6 broadcast_in_dim.10
  3.2 3.2 %reshape.44 = pred[1024,1024]{0,1:T(8,128)(4,1)S(1)} reshape(pred[16,64,16,64]{1,0,3,2:T(8,128)(4,1)S(1)} %broadcast_in_dim.10) | data formatting | bytes 2097152 | tf_op jit(solution)/shard_map/reshape | solution.py:49
  6.4 2.2 %fusion.1.allowed = bf16[1024,1024]{1,0:T(8,128)(2,1)} fusion(pred[1024,1024]{0,1:T(8,128)(4,1)S(1)} %reshape.44, s32[1024]{0:T(1024)S(1)} %add.31), kind=kLoop, calls=%fused_computation.4 | loop fusion | flops 3145728 | bytes 3149824 | tf_op jit(solution)/shard_map/convert_element_type | solution.py:512
  8.5 78.3 %gather.1 = (bf16[1024,128]{1,0:T(8,128)(2,1)}, bf16[1024,128]{1,0:T(8,128)(2,1)}, bf16[1024,128]{1,0:T(8,128)(2,1)}, bf16[1024,2048]{1,0:T(8,128)(2,1)}, bf16[1024,2048]{1,0:T(8,128)(2,1)}) custom-call(bf16[128,1024]{1,0:T(8,128)(2,1)} %bitcast.24, bf16[128,1024]{1,0:T(8,128)(2,1)} %bitcast.25, bf16[128,1024]{1,0:T(8,128)(2,1)} %bitcast.26, ...), custom_call_target="tpu_custom_call" | custom-call | tf_op jit(solution)/shard_map/gather/pallas_call | solution.py:490
  86.9 4.3 %convolution_convert_fusion.2.ga = bf16[1024,128]{1,0:T(8,128)(2,1)} fusion(bf16[1024,2048]{1,0:T(8,128)(2,1)} %get-tuple-element.22, bf16[1024,2048]{1,0:T(8,128)(2,1)} %get-tuple-element.23, s32[]{:T(128)S(6)} %select_n.3), kind=kOutput, calls=%fused_computation.5 | convolution fusion | flops 537001984 | bytes 4980740 | tf_op jit(solution)/shard_map/dot_general | solution.py:504
  91.2 9.3 %attention.1 = (bf16[1024,128]{1,0:T(8,128)(2,1)}, bf16[1024,128]{1,0:T(8,128)(2,1)}, bf16[1024,128]{1,0:T(8,128)(2,1)}, bf16[1024,128]{1,0:T(8,128)(2,1)}) custom-call(bf16[1024,128]{1,0:T(8,128)(2,1)} %get-tuple-element.19.q, bf16[1024,128]{1,0:T(8,128)(2,1)} %get-tuple-element.20.k, bf16[1024,128]{1,0:T(8,128)(2,1)} %get-tuple-element.21.v, ...), custom_call_target="tpu_custom_call" | custom-call | tf_op jit(solution)/shard_map/attention/pallas_call | solution.py:516
  100.4 3.8 %convolution_convert_fusion.1.refs_4_ = bf16[128,2048]{1,0:T(8,128)(2,1)} fusion(bf16[1024,128]{1,0:T(8,128)(2,1)} %get-tuple-element.24.refs_0_, bf16[1024,2048]{1,0:T(8,128)(2,1)} %get-tuple-element.22), kind=kOutput, calls=%fused_computation.2 | convolution fusion | flops 537133056 | bytes 4980736 | tf_op jit(solution)/shard_map/dot_general | solution.py:527
  104.2 29.7 %scatter.1 = (bf16[128,1024]{1,0:T(8,128)(2,1)}, bf16[128,1024]{1,0:T(8,128)(2,1)}, bf16[128,1024]{1,0:T(8,128)(2,1)}, bf16[128,1024]{1,0:T(8,128)(2,1)}, bf16[4,32,2048]{2,1,0:T(8,128)(2,1)}) custom-call(bf16[1024,128]{1,0:T(8,128)(2,1)} %get-tuple-element.24.refs_0_, bf16[1024,128]{1,0:T(8,128)(2,1)} %get-tuple-element.25.refs_1_, ...), custom_call_target="tpu_custom_call" | custom-call | tf_op jit(solution)/shard_map/scatter/pallas_call | solution.py:530
  134.0 0.0 copy-start
  134.0 0.0 copy-start.3
  134.0 0.0 copy-start.2
  134.0 0.0 copy-start.1
  134.0 3.9 %fusion = bf16[1,128,2048]{2,1,0:T(8,128)(2,1)} fusion(bf16[128,1024]{1,0:T(8,128)(2,1)} %get-tuple-element.28, bf16[1024,2048]{1,0:T(8,128)(2,1)} %get-tuple-element.23), kind=kOutput, calls=%fused_computation.3 | convolution fusion | flops 537133056 | bytes 4980736 | tf_op jit(solution)/shard_map/dot_general | solution.py:539
  137.9 0.0 copy-done
  137.9 0.8 convert_reduce_fusion
  138.7 0.0 copy-done.3
  138.7 0.7 copy.16
  139.4 0.7 copy.17
  140.1 0.7 copy.18
  (2 shorter events, 0.0 us)
Async XLA Ops:
  134.0 3.9 %copy-start = (bf16[4,32,2048]{2,1,0:T(8,128)(2,1)S(1)}, bf16[4,32,2048]{2,1,0:T(8,128)(2,1)}, u32[]{:S(2)}) copy-start(bf16[4,32,2048]{2,1,0:T(8,128)(2,1)} %get-tuple-element.32) | copy-start | bytes 1572868
  134.0 4.7 %copy-start.3 = (bf16[128,1024]{1,0:T(8,128)(2,1)S(1)}, bf16[128,1024]{1,0:T(8,128)(2,1)}, u32[]{:S(2)}) copy-start(bf16[128,1024]{1,0:T(8,128)(2,1)} %get-tuple-element.29) | copy-start | bytes 786436
  134.0 5.4 %copy-start.2 = (bf16[128,1024]{1,0:T(8,128)(2,1)S(1)}, bf16[128,1024]{1,0:T(8,128)(2,1)}, u32[]{:S(2)}) copy-start(bf16[128,1024]{1,0:T(8,128)(2,1)} %get-tuple-element.30) | copy-start | bytes 786436
  134.0 6.1 %copy-start.1 = (bf16[128,1024]{1,0:T(8,128)(2,1)S(1)}, bf16[128,1024]{1,0:T(8,128)(2,1)}, u32[]{:S(2)}) copy-start(bf16[128,1024]{1,0:T(8,128)(2,1)} %get-tuple-element.31) | copy-start | bytes 786436

commit v2 on v0

--- a/solution.py
+++ b/solution.py
@@ -3,6 +3,8 @@
 import jax
 import jax.numpy as jnp
 from jax import lax
+from jax.experimental import pallas as pl
+from jax.experimental.pallas import tpu as pltpu
 from jax.sharding import PartitionSpec as P
 
 HEADS = 8
@@ -233,9 +235,329 @@
     )
 
 
+MESH = pl.DeviceIdType.MESH
+
+
+def remote(src, dst, send_sem, recv_sem, device):
+    return pltpu.make_async_remote_copy(
+        src_ref=src,
+        dst_ref=dst,
+        send_sem=send_sem,
+        recv_sem=recv_sem,
+        device_id=device,
+        device_id_type=MESH,
+    )
+
+
+def rows_of(begin, count):
+    return pl.ds(pl.multiple_of(begin, count), count)
+
+
+def greet(devices):
+    barrier = pltpu.get_barrier_semaphore()
+    for device in devices:
+        pl.semaphore_signal(barrier, inc=1, device_id=device, device_id_type=MESH)
+    pl.semaphore_wait(barrier, len(devices))
+
+
+def layer_kernel(
+    n, q, k, v, up, w, allowed, proj, dq, dk, dv, wg,
+    qh, kh, vh, ups, wall, prob, att, attended, dqh, dkh, dvh, dk_sum, dv_sum, dw_sum, dw, dwr,
+    kt, vt, local_sem, heads_s, heads_r, out_s, out_r, ring_s, ring_r,
+    part_s, part_r, cross_s, cross_r, relay_s, relay_r, ws, wr,
+):
+    me = lax.axis_index("cp")
+    col = lax.axis_index("fsdp")
+    partner = {"fsdp": col + 1 - 2 * lax.rem(col, 2)}
+    cross_col = lax.rem(col + 2, 4)
+    cross = {"fsdp": cross_col}
+    tokens = up.shape[0]
+    half = tokens // 2
+    slab = w.shape[0]
+    depth = n // 2
+    zed, why = me // 2, lax.rem(me, 2)
+    place = zed + why * (n - 1 - 2 * zed)
+
+    def at_place(offset):
+        r = lax.rem(place + offset + 2 * n, n)
+        return 2 * r + (r // depth) * (2 * n - 1 - 4 * r)
+
+    def head_cols(d):
+        return rows_of(d * HEAD, HEAD)
+
+    peers = [{"cp": lax.rem(me + i, n)} for i in range(1, n)]
+    columns = [{"fsdp": lax.rem(col + j, 4)} for j in range(1, 4)]
+    greet(peers + columns)
+
+    def chunk_ref(which, owner):
+        if which == 2:
+            return wall.at[rows_of(owner * (4 * slab) + col * slab, slab)]
+        return ups.at[rows_of(owner * tokens + which * half, half)]
+
+    def own_ref(which):
+        if which == 2:
+            return w
+        return up.at[rows_of(which * half, half)]
+
+    sends = []
+    toward = ({"cp": at_place(1)}, {"cp": at_place(-1)})
+
+    def chunks_at(step, way):
+        if step < depth:
+            return (2, 0, 1)
+        return (2, 0) if way == 0 else (1,)
+
+    def ring_start(step, way, which):
+        owner = at_place((1 - step) if way == 0 else (step - 1))
+        source = own_ref(which) if step == 1 else chunk_ref(which, owner)
+        copy = remote(
+            source, chunk_ref(which, owner),
+            ring_s.at[way, step, which], ring_r.at[way, step, which], toward[way],
+        )
+        copy.start()
+        sends.append(copy)
+
+    def ring_wait(step, way, which):
+        owner = at_place(-step if way == 0 else step)
+        block = chunk_ref(which, owner)
+        remote(
+            block, block, ring_s.at[way, step, which], ring_r.at[way, step, which], toward[way]
+        ).wait_recv()
+
+    spread = []
+
+    def spread_weight(owner, source):
+        slot = len(spread)
+        spread.append(owner)
+        block = chunk_ref(2, owner)
+        for device, ss, rs in ((cross, cross_s, cross_r), (partner, part_s, part_r)):
+            copy = remote(source, block, ss.at[slot], rs.at[slot], device)
+            copy.start()
+            sends.append(copy)
+
+    for way in range(2):
+        for which in chunks_at(1, way):
+            ring_start(1, way, which)
+    triples = ((q, qh), (k, kh), (v, vh))
+    for i in range(1, n):
+        d = lax.rem(me + i, n)
+        for t, (a, b) in enumerate(triples):
+            copy = remote(
+                a.at[:, head_cols(d)], b.at[rows_of(me * tokens, tokens)],
+                heads_s.at[t, i], heads_r.at[t, i], {"cp": d},
+            )
+            copy.start()
+            sends.append(copy)
+    own = [
+        pltpu.make_async_copy(
+            a.at[:, head_cols(me)], b.at[rows_of(me * tokens, tokens)], local_sem.at[t]
+        )
+        for t, (a, b) in enumerate(triples)
+    ]
+    own.append(pltpu.make_async_copy(up, ups.at[rows_of(me * tokens, tokens)], local_sem.at[3]))
+    own.append(pltpu.make_async_copy(w, chunk_ref(2, me), local_sem.at[4]))
+    for copy in own:
+        copy.start()
+    spread_weight(me, w)
+    bf16, f32 = jnp.bfloat16, jnp.float32
+    nt = (((1,), (1,)), ((), ()))
+    near = partner["fsdp"]
+    far = lax.rem(near + 2, 4)
+
+    def relay(slot):
+        block = wall.at[rows_of(spread[slot] * (4 * slab) + cross_col * slab, slab)]
+        remote(block, block, cross_s.at[slot], cross_r.at[slot], cross).wait_recv()
+        copy = remote(block, block, relay_s.at[slot], relay_r.at[slot], partner)
+        copy.start()
+        sends.append(copy)
+
+    def weight_wait(slot):
+        for other, ss, rs in ((near, part_s, part_r), (far, relay_s, relay_r)):
+            block = wall.at[rows_of(spread[slot] * (4 * slab) + other * slab, slab)]
+            remote(block, block, ss.at[slot], rs.at[slot], partner).wait_recv()
+
+    def advance(step):
+        for way in range(2):
+            for which in chunks_at(step, way):
+                ring_wait(step, way, which)
+                if step < depth and which in chunks_at(step + 1, way):
+                    ring_start(step + 1, way, which)
+                if which == 2:
+                    owner = at_place(-step if way == 0 else step)
+                    spread_weight(owner, chunk_ref(2, owner))
+
+    def out_send(t, i, source, target):
+        d = lax.rem(me + i, n)
+        copy = remote(
+            source.at[rows_of(d * tokens, tokens)], target.at[:, head_cols(me)],
+            out_s.at[t, i], out_r.at[t, i], {"cp": d},
+        )
+        copy.start()
+        sends.append(copy)
+
+    def out_wait(t, target):
+        for i in range(1, n):
+            source = lax.rem(me + n - i, n)
+            block = target.at[:, head_cols(source)]
+            remote(block, block, out_s.at[t, i], out_r.at[t, i], {"cp": source}).wait_recv()
+
+    advance(1)
+    relay(0)
+    for i in range(1, n):
+        source = lax.rem(me + n - i, n)
+        for t, (a, b) in enumerate(triples):
+            block = b.at[rows_of(source * tokens, tokens)]
+            remote(block, block, heads_s.at[t, i], heads_r.at[t, i], {"cp": source}).wait_recv()
+    for copy in own:
+        copy.wait()
+    kt[...] = kh[...].astype(f32).T.astype(bf16)
+    vt[...] = vh[...].astype(f32).T.astype(bf16)
+    dk_sum[...] = jnp.zeros_like(dk_sum)
+    dv_sum[...] = jnp.zeros_like(dv_sum)
+    dw_sum[...] = jnp.zeros_like(dw_sum)
+
+    def forward(o, carry):
+        rows = rows_of(o * tokens, tokens)
+        scores = lax.dot_general(kh[...], qh[rows], nt, preferred_element_type=f32) * (1.0 / HEAD)
+        scores = jnp.where(allowed[:, rows].astype(f32) > 0.5, scores, lowest)
+        terms = jnp.exp(scores - scores.max(0, keepdims=True))
+        probability = terms * (1.0 / terms.sum(0, keepdims=True))
+        prob[:, rows] = probability
+        att_t = jnp.dot(vt[...], probability.astype(bf16), preferred_element_type=f32)
+        att[rows] = att_t.T.astype(bf16)
+        return carry
+
+    lax.fori_loop(0, n, forward, 0)
+    weight_wait(0)
+    for i in range(1, n):
+        out_send(0, i, att, attended)
+    attended[:, head_cols(me)] = att[rows_of(me * tokens, tokens)]
+
+    def backward(o):
+        rows = rows_of(o * tokens, tokens)
+        up_rows = ups[rows]
+        ga = lax.dot_general(
+            up_rows, wall[rows_of(me * HEAD, HEAD)], nt, preferred_element_type=f32
+        ).astype(bf16)
+        att_rows = att[rows]
+        delta = (att_rows.astype(f32) * ga.astype(f32)).T.sum(0, keepdims=True)
+        dprob = lax.dot_general(vh[...], ga, nt, preferred_element_type=f32)
+        probability = prob[:, rows]
+        ds = (probability * (dprob - delta) * (1.0 / HEAD)).astype(bf16)
+        dqh[rows] = jnp.dot(kt[...], ds, preferred_element_type=f32).T.astype(bf16)
+        dk_sum[...] += jnp.dot(ds, qh[rows], preferred_element_type=f32)
+        dv_sum[...] += jnp.dot(probability.astype(bf16), ga, preferred_element_type=f32)
+        dw_sum[...] += lax.dot_general(
+            att_rows, up_rows, (((0,), (0,)), ((), ())), preferred_element_type=f32
+        )
+
+    backward(me)
+    for step in range(2, depth + 1):
+        advance(step)
+        for slot in range(2 * step - 3, 2 * step - 1):
+            relay(slot)
+        backward(at_place(1 - step))
+        backward(at_place(step - 1))
+    backward(at_place(depth))
+    dkh[...] = dk_sum[...].astype(bf16)
+    dvh[...] = dv_sum[...].astype(bf16)
+    dw[...] = dw_sum[...].astype(bf16)
+    triples_out = ((dkh, dk), (dvh, dv), (dqh, dq))
+    mine = rows_of(me * tokens, tokens)
+    for t, (a, b) in enumerate(triples_out):
+        b[:, head_cols(me)] = a[mine]
+        for i in range(1, n):
+            out_send(t + 1, i, a, b)
+    for j in range(1, 4):
+        g = lax.rem(col + j, 4)
+        copy = remote(dw.at[rows_of(g * slab, slab)], dwr.at[j], ws.at[j], wr.at[j], {"fsdp": g})
+        copy.start()
+        sends.append(copy)
+    relay(len(spread) - 1)
+    for slot in range(1, len(spread)):
+        weight_wait(slot)
+    out_wait(0, attended)
+    width = math.gcd(proj.shape[1], 512)
+
+    def project(i, carry):
+        cols = rows_of(i * width, width)
+        proj[:, cols] = jnp.dot(
+            attended[...], wall[:, cols], preferred_element_type=f32
+        ).astype(bf16)
+        return carry
+
+    lax.fori_loop(0, proj.shape[1] // width, project, 0)
+    for j in range(1, 4):
+        block = dwr.at[j]
+        remote(block, block, ws.at[j], wr.at[j], columns[j - 1]).wait_recv()
+    total = dw[rows_of(col * slab, slab)].astype(f32)
+    for j in range(1, 4):
+        total = total + dwr[j].astype(f32)
+    wg[...] = total
+    for t, (a, b) in enumerate(triples_out):
+        out_wait(t + 1, b)
+    for copy in sends:
+        copy.wait_send()
+
+
+def by_heads(query_states, key_states, value_states, span_order, block_mask, output_weight, upstream):
+    n = lax.axis_size("cp")
+    m = lax.axis_size("fsdp")
+    tokens, width = query_states.shape[1:]
+    length = tokens * n
+    model = upstream.shape[2]
+    slab = output_weight.shape[0]
+    span_rows = tokens // 2
+    bf16, f32 = jnp.bfloat16, jnp.float32
+    shape = jax.ShapeDtypeStruct
+    vmem = pl.BlockSpec(memory_space=pltpu.VMEM)
+    dma = pltpu.SemaphoreType.DMA
+    half = n // 2
+    positions = (
+        span_order[:, None] * span_rows + jnp.arange(span_rows, dtype=jnp.int32)[None, :]
+    ).reshape(-1)
+    spans = span_order.shape[0]
+    member = (
+        jnp.arange(length, dtype=jnp.int32)[:, None] // span_rows
+        == jnp.arange(spans, dtype=jnp.int32)[None, :]
+    ).astype(bf16)
+    span_ok = storage_mask(span_order, block_mask).astype(bf16)
+    key_side = lax.dot_general(member, span_ok, (((1,), (1,)), ((), ())), preferred_element_type=bf16)
+    seen = lax.dot_general(key_side, member, (((1,), (1,)), ((), ())), preferred_element_type=f32)
+    allowed = ((seen > 0.5) & (positions[:, None] <= positions[None, :])).astype(bf16)
+    head_array = pltpu.VMEM((length, HEAD), bf16)
+    head_sum = pltpu.VMEM((length, HEAD), f32)
+    projected, dq, dk, dv, weight_gradient = pl.pallas_call(
+        lambda *refs: layer_kernel(n, *refs),
+        out_shape=(shape((tokens, model), bf16),)
+        + (shape((tokens, width), bf16),) * 3
+        + (shape((slab, model), f32),),
+        in_specs=[vmem] * 6,
+        out_specs=(vmem,) * 5,
+        scratch_shapes=[
+            head_array, head_array, head_array,
+            pltpu.VMEM((length, model), bf16), pltpu.VMEM((width, model), bf16),
+            pltpu.VMEM((length, length), f32), head_array, pltpu.VMEM((tokens, width), bf16),
+            head_array, head_array, head_array, head_sum, head_sum,
+            pltpu.VMEM((HEAD, model), f32), pltpu.VMEM((HEAD, model), bf16),
+            pltpu.VMEM((m, slab, model), bf16),
+            pltpu.VMEM((HEAD, length), bf16), pltpu.VMEM((HEAD, length), bf16),
+            dma((5,)), dma((3, n)), dma((3, n)), dma((4, n)), dma((4, n)),
+            dma((2, half + 1, 3)), dma((2, half + 1, 3)),
+        ]
+        + [dma((n,))] * 6 + [dma((m,))] * 2,
+        compiler_params=pltpu.CompilerParams(
+            collective_id=0, has_side_effects=True, vmem_limit_bytes=48 << 20
+        ),
+        name="layer",
+    )(query_states[0], key_states[0], value_states[0], upstream[0], output_weight, allowed)
+    return (projected[None], dq[None], dk[None], dv[None], weight_gradient)
+
+
 def solution(mesh):
+    fits = mesh.shape["cp"] == HEADS and mesh.shape["fsdp"] == 4
     return jax.shard_map(
-        local,
+        by_heads if fits else local,
         mesh=mesh,
         in_specs=(
             P("fsdp", "cp", None),

time: 408 us -> 107 us (0.26)
  waiting for transfers between devices: 204 us -> 0 us
  Pallas kernels: 0 us -> 100 us
  blocking collectives: 66 us -> 0 us
  local copies, waits for them, and re-layouts: 59.5 us -> 3.7 us
  matrix products: 43.6 us -> 2.03 us
  between operations: 14.3 us -> 0.73 us
  other arithmetic: 12.9 us -> 0.84 us
  loops' own time: 6.1 us -> 0 us
    all_gather x5 -> x0, waiting for transfers between devices: 181 us -> none  [the longest x1 50 us: local(): lax.all_gather(key_local, 'cp', axis=0, tiled=True)]
    pallas_call x0 -> x1, Pallas kernels: none -> 100 us  [by_heads(): pl.pallas_call(lambda *refs: layer_kernel(n, *refs), out_shape=(shape((to...]
    all_gather x2 -> x0, blocking collectives: 66 us -> none  [the longest x1 33.7 us: local(): lax.all_gather(row_delta, 'cp', axis=0, tiled=True)]
    dot_general x19 -> x1, matrix products: 42.6 us -> 1 us  [by_heads(): lax.dot_general(key_side, member, (((1,), (1,)), ((), ())), preferred_ele...]
    dynamic_slice x37 -> x0, local copies, waits for them, and re-layouts: 27.3 us -> none  [the longest x8 6.01 us: local(): (maxima, totals), _ = lax.scan(stats_step, stat_start, block_steps)]
    reduce_scatter x2 -> x0, waiting for transfers between devices: 22.1 us -> none  [the longest x1 22.1 us: local(): lax.psum_scatter(partial_batch, 'cp', scatter_dimension=0, tiled=True)]
    reshape x12 -> x0, local copies, waits for them, and re-layouts: 7.68 us -> none  [the longest x8 3.07 us: allowed_block(): spread = spread.reshape(query_total, key_total)]
    while x48 -> x0, local copies, waits for them, and re-layouts: 7.25 us -> none
  transfers between devices with their start and end apart: 7 -> 0, of which waited for: 5 -> 0; matrix products, arithmetic and copies ran while one was open for 26% -> 0% of each run, Pallas kernels for 0% -> 0%
where the time goes in v2:
time: 107 us
  Pallas kernels  100 us (93%)
  local copies, waits for them, and re-layouts  3.7 us (3%)
  matrix products  2.03 us (2%)
    pallas_call x1, Pallas kernels, by_heads(): pl.pallas_call(lambda *refs: layer_kernel(n, *refs), out_shape=(shape((to...  100 us
    unnamed x15, local copies, waits for them, and re-layouts  3.63 us

profile of v2, /device:TPU:0, one launch (start us, length us, event | category | flops | bytes accessed | tf_op | source)
XLA Modules:
  0.0 107.3 jit_solution(8982288957657486884)
XLA Ops:
  0.6 0.0 copy-start
  0.6 0.0 copy-start.4
  0.7 0.0 copy-start.3
  0.7 0.0 copy-start.2
  0.7 0.0 copy-start.1
  0.7 0.8 broadcast_multiply_fusion
  1.4 1.0 fusion.5
  2.5 0.1 iota_add_fusion
  2.6 0.1 add.33
  2.6 1.0 and_convert_fusion.refs_5_
  3.6 0.0 copy-done
  3.6 0.0 copy-done.4
  3.6 0.0 copy-done.3
  3.7 0.0 copy-done.2
  3.7 0.0 copy-done.1
  3.7 100.0 %layer.1 = (bf16[128,2048]{1,0:T(8,128)(2,1)S(1)}, bf16[128,1024]{1,0:T(8,128)(2,1)S(1)}, bf16[128,1024]{1,0:T(8,128)(2,1)S(1)}, bf16[128,1024]{1,0:T(8,128)(2,1)S(1)}, f32[32,2048]{1,0:T(8,128)S(1)}) custom-call(bf16[128,1024]{1,0:T(8,128)(2,1)S(1)} %bitcast.11, bf16[128,1024]{1,0:T(8,128)(2,1)S(1)} %bitcast.12, bf16[128,1024]{1,0:T(8,128)(2,1)S(1)} %bitcast.13, ...), custom_call_target="tpu_custom_call" | custom-call | tf_op jit(solution)/shard_map/layer/pallas_call | solution.py:530
  103.7 0.8 copy.17
  104.5 0.7 copy.18
  105.2 0.7 copy.19
  105.9 0.7 copy.20
  106.6 0.7 copy.21
  (1 shorter events, 0.0 us)
Async XLA Ops:
  0.6 3.0 %copy-start = (bf16[1,128,2048]{2,1,0:T(8,128)(2,1)S(1)}, bf16[1,128,2048]{2,1,0:T(8,128)(2,1)}, u32[]{:S(2)}) copy-start(bf16[1,128,2048]{2,1,0:T(8,128)(2,1)} %param.13) | copy-start | bytes 1572868
  0.6 3.0 %copy-start.4 = (bf16[32,2048]{1,0:T(8,128)(2,1)S(1)}, bf16[32,2048]{1,0:T(8,128)(2,1)}, u32[]{:S(2)}) copy-start(bf16[32,2048]{1,0:T(8,128)(2,1)} %refs_4_.1) | copy-start | bytes 393220
  0.7 3.0 %copy-start.3 = (bf16[1,128,1024]{2,1,0:T(8,128)(2,1)S(1)}, bf16[1,128,1024]{2,1,0:T(8,128)(2,1)}, u32[]{:S(2)}) copy-start(bf16[1,128,1024]{2,1,0:T(8,128)(2,1)} %param.9) | copy-start | bytes 786436
  0.7 3.0 %copy-start.2 = (bf16[1,128,1024]{2,1,0:T(8,128)(2,1)S(1)}, bf16[1,128,1024]{2,1,0:T(8,128)(2,1)}, u32[]{:S(2)}) copy-start(bf16[1,128,1024]{2,1,0:T(8,128)(2,1)} %param.8) | copy-start | bytes 786436
  0.7 3.0 %copy-start.1 = (bf16[1,128,1024]{2,1,0:T(8,128)(2,1)S(1)}, bf16[1,128,1024]{2,1,0:T(8,128)(2,1)}, u32[]{:S(2)}) copy-start(bf16[1,128,1024]{2,1,0:T(8,128)(2,1)} %param.7) | copy-start | bytes 786436

commit v3 on v2

--- a/solution.py
+++ b/solution.py
@@ -376,9 +376,11 @@
             block = wall.at[rows_of(spread[slot] * (4 * slab) + other * slab, slab)]
             remote(block, block, ss.at[slot], rs.at[slot], partner).wait_recv()
 
-    def advance(step):
-        for way in range(2):
-            for which in chunks_at(step, way):
+    def advance(step, chunks):
+        for which in chunks:
+            for way in range(2):
+                if which not in chunks_at(step, way):
+                    continue
                 ring_wait(step, way, which)
                 if step < depth and which in chunks_at(step + 1, way):
                     ring_start(step + 1, way, which)
@@ -401,7 +403,7 @@
             block = target.at[:, head_cols(source)]
             remote(block, block, out_s.at[t, i], out_r.at[t, i], {"cp": source}).wait_recv()
 
-    advance(1)
+    advance(1, (2, 0, 1))
     relay(0)
     for i in range(1, n):
         source = lax.rem(me + n - i, n)
@@ -451,12 +453,25 @@
             att_rows, up_rows, (((0,), (0,)), ((), ())), preferred_element_type=f32
         )
 
+    def query_send(o):
+        i = lax.rem(o + n - me, n)
+        copy = remote(
+            dqh.at[rows_of(o * tokens, tokens)], dq.at[:, head_cols(me)],
+            out_s.at[3, i], out_r.at[3, i], {"cp": o},
+        )
+        copy.start()
+        sends.append(copy)
+
     backward(me)
     for step in range(2, depth + 1):
-        advance(step)
-        for slot in range(2 * step - 3, 2 * step - 1):
-            relay(slot)
+        advance(step, (2, 0))
+        if step > 2:
+            for offset in (2 - step, step - 2):
+                query_send(at_place(offset))
+        relay(2 * step - 3)
         backward(at_place(1 - step))
+        advance(step, (1,))
+        relay(2 * step - 2)
         backward(at_place(step - 1))
     backward(at_place(depth))
     dkh[...] = dk_sum[...].astype(bf16)
@@ -466,8 +481,11 @@
     mine = rows_of(me * tokens, tokens)
     for t, (a, b) in enumerate(triples_out):
         b[:, head_cols(me)] = a[mine]
-        for i in range(1, n):
-            out_send(t + 1, i, a, b)
+        if t < 2:
+            for i in range(1, n):
+                out_send(t + 1, i, a, b)
+    for offset in (1 - depth, depth - 1, depth):
+        query_send(at_place(offset))
     for j in range(1, 4):
         g = lax.rem(col + j, 4)
         copy = remote(dw.at[rows_of(g * slab, slab)], dwr.at[j], ws.at[j], wr.at[j], {"fsdp": g})

time: 107 us -> 107 us (level)
  no operation moved by 1% of the time
where the time goes in v3:
time: 107 us
  Pallas kernels  99.4 us (93%)
  local copies, waits for them, and re-layouts  3.7 us (3%)
  matrix products  2.03 us (2%)
    pallas_call x1, Pallas kernels, by_heads(): pl.pallas_call(lambda *refs: layer_kernel(n, *refs), out_shape=(shape((to...  99.4 us
    unnamed x15, local copies, waits for them, and re-layouts  3.63 us

profile of v3, /device:TPU:0, one launch (start us, length us, event | category | flops | bytes accessed | tf_op | source)
XLA Modules:
  0.0 106.7 jit_solution(15024164037865930722)
XLA Ops:
  0.6 0.0 copy-start
  0.6 0.0 copy-start.4
  0.7 0.0 copy-start.3
  0.7 0.0 copy-start.2
  0.7 0.0 copy-start.1
  0.7 0.8 broadcast_multiply_fusion
  1.4 1.0 fusion.5
  2.5 0.1 iota_add_fusion
  2.6 0.1 add.33
  2.6 1.0 and_convert_fusion.refs_5_
  3.6 0.0 copy-done
  3.6 0.0 copy-done.4
  3.6 0.0 copy-done.3
  3.7 0.0 copy-done.2
  3.7 0.0 copy-done.1
  3.7 99.4 %layer.1 = (bf16[128,2048]{1,0:T(8,128)(2,1)S(1)}, bf16[128,1024]{1,0:T(8,128)(2,1)S(1)}, bf16[128,1024]{1,0:T(8,128)(2,1)S(1)}, bf16[128,1024]{1,0:T(8,128)(2,1)S(1)}, f32[32,2048]{1,0:T(8,128)S(1)}) custom-call(bf16[128,1024]{1,0:T(8,128)(2,1)S(1)} %bitcast.11, bf16[128,1024]{1,0:T(8,128)(2,1)S(1)} %bitcast.12, bf16[128,1024]{1,0:T(8,128)(2,1)S(1)} %bitcast.13, ...), custom_call_target="tpu_custom_call" | custom-call | tf_op jit(solution)/shard_map/layer/pallas_call | solution.py:548
  103.1 0.8 copy.17
  103.9 0.7 copy.18
  104.6 0.7 copy.19
  105.3 0.7 copy.20
  106.0 0.7 copy.21
  (1 shorter events, 0.0 us)
Async XLA Ops:
  0.6 3.0 %copy-start = (bf16[1,128,2048]{2,1,0:T(8,128)(2,1)S(1)}, bf16[1,128,2048]{2,1,0:T(8,128)(2,1)}, u32[]{:S(2)}) copy-start(bf16[1,128,2048]{2,1,0:T(8,128)(2,1)} %param.13) | copy-start | bytes 1572868
  0.6 3.0 %copy-start.4 = (bf16[32,2048]{1,0:T(8,128)(2,1)S(1)}, bf16[32,2048]{1,0:T(8,128)(2,1)}, u32[]{:S(2)}) copy-start(bf16[32,2048]{1,0:T(8,128)(2,1)} %refs_4_.1) | copy-start | bytes 393220
  0.7 3.0 %copy-start.3 = (bf16[1,128,1024]{2,1,0:T(8,128)(2,1)S(1)}, bf16[1,128,1024]{2,1,0:T(8,128)(2,1)}, u32[]{:S(2)}) copy-start(bf16[1,128,1024]{2,1,0:T(8,128)(2,1)} %param.9) | copy-start | bytes 786436
  0.7 3.0 %copy-start.2 = (bf16[1,128,1024]{2,1,0:T(8,128)(2,1)S(1)}, bf16[1,128,1024]{2,1,0:T(8,128)(2,1)}, u32[]{:S(2)}) copy-start(bf16[1,128,1024]{2,1,0:T(8,128)(2,1)} %param.8) | copy-start | bytes 786436
  0.7 3.0 %copy-start.1 = (bf16[1,128,1024]{2,1,0:T(8,128)(2,1)S(1)}, bf16[1,128,1024]{2,1,0:T(8,128)(2,1)}, u32[]{:S(2)}) copy-start(bf16[1,128,1024]{2,1,0:T(8,128)(2,1)} %param.7) | copy-start | bytes 786436
